TPU v7x, 128 devices: a whole 4x4x4 slice. The times are simulated.
128 devices in a mesh: gx: 4 (over z_hi, core), gy: 4 (over y), gz: 8 (over z_lo, x).
Axes of the slice: x: 4, y: 4, z: 4 (z_hi: 2, z_lo: 2; z = z_hi * 2 + z_lo), core: 2. Of those that a mesh axis runs over, the one named last changes fastest.
Arguments:
- grads: bfloat16 [8, 2048, 3584], P('gz', ('gx', 'gy')), may hold values from -300 to 300
- momentum: float32 [2048, 3584], P(('gx', 'gy')), may hold values from -0.8 to 0.8
- variance: float32 [2048, 3584], P(('gx', 'gy'), 'gz'), may hold values from 0.25 to 4
- master: float32 [2048, 3584], P(('gx', 'gy', 'gz')), may hold values from -6 to 6
Outputs:
- weights: bfloat16 [2048, 3584], replicated
- new_master: float32 [2048, 3584], P(('gx', 'gy', 'gz'))
- new_momentum: float32 [2048, 3584], P(('gx', 'gy', 'gz'))
- worker_error: float32 [8, 2048, 3584], P('gz', ('gx', 'gy'))
All inputs are finite; a program needn't handle non-finite values.
Results may differ from a plain program's by a relative error of at most 0.007.
Values may be sent and summed in bfloat16 or wider, within the bound.
A program may use at most 128 MiB of HBM per device.

v0:
```python
import jax
import jax.numpy as jnp
from jax import lax
from jax.sharding import PartitionSpec as P

beta_one = 0.9
learning_rate = 0.25
epsilon = 1e-08


def from_everyone(x, axis):
    copies = jnp.broadcast_to(x, (lax.axis_size(axis), *x.shape))
    return lax.all_to_all(copies, axis, split_axis=0, concat_axis=0, tiled=True)


def joined_along(blocks, dim):
    blocks = jnp.moveaxis(blocks, 0, dim)
    shape = blocks.shape
    return blocks.reshape(*shape[:dim], shape[dim] * shape[dim + 1], *shape[dim + 2 :])


def collect(x, axis, dim):
    blocks = from_everyone(x, axis)
    return joined_along(blocks, dim)


def shards(grads, momentum, variance, master):
    owned_variance = lax.all_to_all(
        variance.astype(jnp.bfloat16), "gz", split_axis=0, concat_axis=1, tiled=True
    ).astype(variance.dtype)
    corrected = beta_one * momentum + (1.0 - beta_one) * grads[0].astype(jnp.float32)
    level = jnp.mean(jnp.abs(corrected), axis=-1, keepdims=True).astype(jnp.bfloat16)
    signs = jnp.where(corrected >= 0.0, 1.0, -1.0).astype(jnp.float32)
    compressed = (level.astype(jnp.float32) * signs).astype(jnp.bfloat16)
    worker_error = (corrected - compressed.astype(jnp.float32))[None]
    received = lax.all_to_all(compressed[:, None, :], "gz", split_axis=0, concat_axis=1, tiled=True)
    new_momentum = jnp.sum(received.astype(jnp.float32), axis=1) / received.shape[1]
    new_master = master - learning_rate * new_momentum / (jnp.sqrt(owned_variance) + epsilon)
    shard = new_master.astype(jnp.bfloat16)
    gathered = collect(shard, "gz", 0)
    weights = lax.all_gather(gathered, ("gx", "gy"), axis=0, tiled=True)
    return (weights, new_master, new_momentum, worker_error)


def solution(mesh):
    return jax.shard_map(
        shards,
        mesh=mesh,
        in_specs=(
            P("gz", ("gx", "gy"), None),
            P(("gx", "gy"), None),
            P(("gx", "gy"), "gz"),
            P(("gx", "gy", "gz"), None),
        ),
        out_specs=(
            P(),
            P(("gx", "gy", "gz"), None),
            P(("gx", "gy", "gz"), None),
            P("gz", ("gx", "gy"), None),
        ),
        check_vma=False,
    )
```

profile of v0, /device:TPU:1, one launch (start us, length us, event | category | flops | bytes accessed | tf_op | source)
XLA Modules:
  0.0 189.1 jit_solution(6112298998503527955)
XLA Ops:
  7.2 0.0 copy-start
  7.2 0.0 copy-start.1
  7.2 1.8 copy.15
  9.0 6.2 %all-to-all-start.1 = ((bf16[8,16,448]{2,1,0:T(8,128)(2,1)}), bf16[8,16,448]{2,1,0:T(8,128)(2,1)S(1)}, u32[]{:S(2)}, u32[]{:S(2)}) async-start(bf16[8,16,448]{2,1,0:T(8,128)(2,1)} %bitcast.2), calls=%async_computation.1 | async-start | bytes 262144 | tf_op jit(solution)/shard_map/all_to_all | solution.py:28
  15.2 2.2 %abs_reduce_fusion = f32[128]{0:T(128)S(1)} fusion(bf16[1,128,3584]{2,1,0:T(8,128)(2,1)} %param.4, f32[128,3584]{1,0:T(8,128)} %param.5), kind=kLoop, calls=%fused_computation.3 | loop fusion | flops 2752384 | bytes 2753024 | tf_op jit(solution)/shard_map/reduce_sum | solution.py:32
  17.5 0.0 copy-done
  17.5 0.0 copy-done.1
  17.5 2.1 %subtract_bitcast_fusion = (f32[1,128,3584]{2,1,0:T(8,128)}, bf16[128,1,3584]{2,0,1:T(8,128)(2,1)}) fusion(f32[128]{0:T(128)S(1)} %convert_convert_fusion, bf16[1,128,3584]{2,1,0:T(8,128)(2,1)S(1)} %copy-done.1, f32[128,3584]{1,0:T(8,128)S(1)} %copy-done), kind=kLoop, calls=%fused_computation.1 | loop fusion | flops 4587520 | bytes 5505536 | tf_op jit(solution)/shard_map/broadcast_in_dim | solution.py:35
  19.5 0.5 broadcast.14
  20.0 2.5 %reduce.3 = bf16[128,3584]{1,0:T(8,128)(2,1)S(1)} reduce(bf16[128,1,3584]{2,0,1:T(8,128)(2,1)} %get-tuple-element.7, bf16[]{:T(256)} %broadcast.14), dimensions={1}, to_apply=%copy.14.reduce_sub_computation | reduce | bytes 1835010 | tf_op jit(solution)/shard_map/broadcast_in_dim | solution.py:36
  22.5 1.6 reshape.35
  24.1 0.0 all-to-all-done.1
  24.1 5.1 %all-to-all-start = ((bf16[8,2,28672]{2,1,0:T(2,128)(2,1)}), bf16[8,2,28672]{2,1,0:T(2,128)(2,1)S(1)}, u32[]{:S(2)}, u32[]{:S(2)}) async-start(bf16[8,2,28672]{2,1,0:T(2,128)(2,1)} %reshape.35), calls=%async_computation | async-start | bytes 1835008 | tf_op jit(solution)/shard_map/all_to_all | solution.py:36
  29.3 0.0 all-gather.2.cloned.1.call-start
  29.3 0.1 add_bitcast_fusion
  29.4 0.2 copy.16
  29.6 0.1 add.19
  29.7 14.0 %all-to-all-done = bf16[8,2,28672]{2,1,0:T(2,128)(2,1)S(1)} async-done(((bf16[8,2,28672]{2,1,0:T(2,128)(2,1)}), bf16[8,2,28672]{2,1,0:T(2,128)(2,1)S(1)}, u32[]{:S(2)}, u32[]{:S(2)}) %all-to-all-start) | async-done | bytes 917536 | tf_op jit(solution)/shard_map/all_to_all | solution.py:36
  43.7 3.3 %reshape.36 = bf16[128,1,3584]{2,1,0:T(2,128)(2,1)} reshape(bf16[8,2,28672]{2,1,0:T(2,128)(2,1)S(1)} %all-to-all-done) | data formatting | bytes 1835008
  47.0 1.6 copy.17
  48.6 0.0 copy-start.2
  48.7 0.1 reduce_sum.19
  48.8 0.8 copy-done.2
  49.6 0.8 fusion.1
  50.4 0.1 broadcast_in_dim.21
  50.5 17.1 %all_to_all.27 = bf16[8,16,3584]{2,1,0:T(8,128)(2,1)} all-to-all(bf16[8,16,3584]{2,1,0:T(8,128)(2,1)S(1)} %broadcast_in_dim.21), channel_id=1, replica_groups=mesh['gx'=4,'gy'=4,'gz'=8] {'gz'}, dimensions={0} | all-to-all | bytes 1835008 | tf_op jit(solution)/shard_map/all_to_all | solution.py:13
  67.5 0.0 all-gather.2.cloned.1.call-update
  67.6 101.6 %all-gather.2.cloned.1.call-done = bf16[2048,3584]{1,0:T(8,128)(2,1)} async-done(((bf16[128,3584]{1,0:T(8,128)(2,1)}), bf16[2048,3584]{1,0:T(8,128)(2,1)}) %all-gather.2.cloned.1.call-update) | async-done | bytes 14680080 | tf_op jit(solution)/shard_map/all_gather | solution.py:41
  169.2 13.1 %copy.20 = bf16[2048,3584]{1,0:T(8,128)(2,1)} copy(bf16[2048,3584]{1,0:T(8,128)(2,1)} %all-gather.2.cloned.1.call-done) | data formatting | bytes 29360128
  (1 shorter events, 0.0 us)
Async XLA Ops:
  7.2 10.3 %copy-start = (f32[128,3584]{1,0:T(8,128)S(1)}, f32[128,3584]{1,0:T(8,128)}, u32[]{:S(2)}) copy-start(f32[128,3584]{1,0:T(8,128)} %param.5) | copy-start | bytes 5505028
  7.2 10.3 %copy-start.1 = (bf16[1,128,3584]{2,1,0:T(8,128)(2,1)S(1)}, bf16[1,128,3584]{2,1,0:T(8,128)(2,1)}, u32[]{:S(2)}) copy-start(bf16[1,128,3584]{2,1,0:T(8,128)(2,1)} %param.4) | copy-start | bytes 2752516
  9.0 15.1 %all-to-all-start.1 = ((bf16[8,16,448]{2,1,0:T(8,128)(2,1)}), bf16[8,16,448]{2,1,0:T(8,128)(2,1)S(1)}, u32[]{:S(2)}, u32[]{:S(2)}) async-start(bf16[8,16,448]{2,1,0:T(8,128)(2,1)} %bitcast.2), calls=%async_computation.1 | async-start | bytes 262144 | tf_op jit(solution)/shard_map/all_to_all | solution.py:28
  24.1 19.6 %all-to-all-start = ((bf16[8,2,28672]{2,1,0:T(2,128)(2,1)}), bf16[8,2,28672]{2,1,0:T(2,128)(2,1)S(1)}, u32[]{:S(2)}, u32[]{:S(2)}) async-start(bf16[8,2,28672]{2,1,0:T(2,128)(2,1)} %reshape.35), calls=%async_computation | async-start | bytes 1835008 | tf_op jit(solution)/shard_map/all_to_all | solution.py:36
  29.3 139.9 %all-gather.2.cloned.1.call-start = ((), (), s32[]{:S(2)}) async-start(), calls=%async_computation.3 | async-start | bytes 15597568 | tf_op jit(solution)/shard_map/all_gather | solution.py:41
  48.6 0.9 copy-start.2
Sparse Core Ops, SparseCore 0:
  67.7 101.4 all-gather.1
where the time goes:
time: 190 us; the launch traced here: 189 us
  waiting for transfers between devices  116 us (61%)
  local copies, waits for them, and re-layouts  23.2 us (12%)
  blocking collectives  17.1 us (9%)
  between operations  14.1 us (7%)
  starting transfers between devices  11.4 us (6%)
  other arithmetic  7.75 us (4%)
    all_gather x1, waiting for transfers between devices, shards(): weights = lax.all_gather(gathered, ('gx', 'gy'), axis=0, tiled=True)  102 us
    unnamed x11, local copies, waits for them, and re-layouts  22.3 us
    all_to_all x1, blocking collectives, from_everyone(): return lax.all_to_all(copies, axis, split_axis=0, concat_axis=0, tiled=True)  17.1 us
    all_to_all x1, waiting for transfers between devices, shards(): lax.all_to_all(compressed[:, None, :], 'gz', split_axis=0, concat_axis=1,...  14 us
    all_to_all x1, starting transfers between devices, shards(): lax.all_to_all(variance.astype(jnp.bfloat16), 'gz', split_axis=0, concat_...  6.19 us
    all_to_all x1, starting transfers between devices, shards(): lax.all_to_all(compressed[:, None, :], 'gz', split_axis=0, concat_axis=1,...  5.14 us
  transfers between devices with their start and end apart: 3, of which 2 were waited for; matrix products, arithmetic and copies ran while one was open for 5% of the time, Pallas kernels for 0%

commit v1 on v0

--- a/solution.py
+++ b/solution.py
@@ -38,7 +38,10 @@
     new_master = master - learning_rate * new_momentum / (jnp.sqrt(owned_variance) + epsilon)
     shard = new_master.astype(jnp.bfloat16)
     gathered = collect(shard, "gz", 0)
-    weights = lax.all_gather(gathered, ("gx", "gy"), axis=0, tiled=True)
+    weights = jnp.concatenate(
+        lax.all_to_all(jnp.stack([gathered] * lax.axis_size(("gx", "gy"))), ("gx", "gy"), 0, 0),
+        axis=0,
+    )
     return (weights, new_master, new_momentum, worker_error)
 
 

time: 190 us -> 246 us (1.29)
  blocking collectives: 17.1 us -> 188 us
  waiting for transfers between devices: 116 us -> 14.1 us
  between operations: 14.1 us -> 0.71 us
    all_to_all x0 -> x1, blocking collectives: none -> 172 us  [shards(): lax.all_to_all(jnp.stack([gathered] * lax.axis_size(('gx', 'gy'))), ('gx'...]
    all_gather x1 -> x0, waiting for transfers between devices: 102 us -> none  [shards(): weights = lax.all_gather(gathered, ('gx', 'gy'), axis=0, tiled=True)]
    unnamed x11, local copies, waits for them, and re-layouts: 22.3 us -> 14.6 us
    another operation x0 -> x1, local copies, waits for them, and re-layouts: none -> 6.88 us  [shards(): jnp.stack([gathered] * lax.axis_size(('gx', 'gy')))]
  transfers between devices with their start and end apart: 3 -> 2, of which waited for: 2 -> 1; matrix products, arithmetic and copies ran while one was open for 5% -> 4% of each run, Pallas kernels for 0% -> 0%
where the time goes in v1:
time: 246 us; the launch traced here: 244 us
  blocking collectives  188 us (76%)
  local copies, waits for them, and re-layouts  22.4 us (9%)
  waiting for transfers between devices  14.1 us (6%)
  starting transfers between devices  11.3 us (5%)
  other arithmetic  7.75 us (3%)
    all_to_all x1, blocking collectives, shards(): lax.all_to_all(jnp.stack([gathered] * lax.axis_size(('gx', 'gy'))), ('gx'...  172 us
    all_to_all x1, blocking collectives, from_everyone(): return lax.all_to_all(copies, axis, split_axis=0, concat_axis=0, tiled=True)  16.2 us
    unnamed x11, local copies, waits for them, and re-layouts  14.6 us
    all_to_all x1, waiting for transfers between devices, shards(): lax.all_to_all(compressed[:, None, :], 'gz', split_axis=0, concat_axis=1,...  14.1 us
    another operation x1, local copies, waits for them, and re-layouts, shards(): jnp.stack([gathered] * lax.axis_size(('gx', 'gy')))  6.88 us
    all_to_all x1, starting transfers between devices, shards(): lax.all_to_all(variance.astype(jnp.bfloat16), 'gz', split_axis=0, concat_...  6.19 us
    all_to_all x1, starting transfers between devices, shards(): lax.all_to_all(compressed[:, None, :], 'gz', split_axis=0, concat_axis=1,...  5.14 us
  transfers between devices with their start and end apart: 2, of which 1 were waited for; matrix products, arithmetic and copies ran while one was open for 4% of the time, Pallas kernels for 0%

profile of v1, /device:TPU:1, one launch (start us, length us, event | category | flops | bytes accessed | tf_op | source)
XLA Modules:
  0.0 244.0 jit_solution(1136089879532882368)
XLA Ops:
  0.6 0.0 copy-start
  0.6 0.0 copy-start.1
  0.7 1.8 copy.15
  2.5 6.2 %all-to-all-start.1 = ((bf16[8,16,448]{2,1,0:T(8,128)(2,1)}), bf16[8,16,448]{2,1,0:T(8,128)(2,1)S(1)}, u32[]{:S(2)}, u32[]{:S(2)}) async-start(bf16[8,16,448]{2,1,0:T(8,128)(2,1)} %bitcast.2), calls=%async_computation.1 | async-start | bytes 262144 | tf_op jit(solution)/shard_map/all_to_all | solution.py:28
  8.7 2.2 abs_reduce_fusion
  10.9 0.0 copy-done
  10.9 0.0 copy-done.1
  10.9 2.1 subtract_bitcast_fusion
  13.0 0.5 broadcast.15
  13.5 2.5 %reduce.3 = bf16[128,3584]{1,0:T(8,128)(2,1)S(1)} reduce(bf16[128,1,3584]{2,0,1:T(8,128)(2,1)} %get-tuple-element.7, bf16[]{:T(256)} %broadcast.15), dimensions={1}, to_apply=%copy.14.reduce_sub_computation | reduce | bytes 1835010 | tf_op jit(solution)/shard_map/broadcast_in_dim | solution.py:36
  16.0 1.6 reshape.37
  17.6 0.0 all-to-all-done.1
  17.6 5.1 %all-to-all-start = ((bf16[8,2,28672]{2,1,0:T(2,128)(2,1)}), bf16[8,2,28672]{2,1,0:T(2,128)(2,1)S(1)}, u32[]{:S(2)}, u32[]{:S(2)}) async-start(bf16[8,2,28672]{2,1,0:T(2,128)(2,1)} %reshape.37), calls=%async_computation | async-start | bytes 1835008 | tf_op jit(solution)/shard_map/all_to_all | solution.py:36
  22.7 0.1 add_bitcast_fusion
  22.8 0.2 copy.16
  23.0 0.1 add.19
  23.1 14.1 %all-to-all-done = bf16[8,2,28672]{2,1,0:T(2,128)(2,1)S(1)} async-done(((bf16[8,2,28672]{2,1,0:T(2,128)(2,1)}), bf16[8,2,28672]{2,1,0:T(2,128)(2,1)S(1)}, u32[]{:S(2)}, u32[]{:S(2)}) %all-to-all-start) | async-done | bytes 917536 | tf_op jit(solution)/shard_map/all_to_all | solution.py:36
  37.2 3.3 %reshape.38 = bf16[128,1,3584]{2,1,0:T(2,128)(2,1)} reshape(bf16[8,2,28672]{2,1,0:T(2,128)(2,1)S(1)} %all-to-all-done) | data formatting | bytes 1835008
  40.5 1.6 copy.17
  42.1 0.0 copy-start.2
  42.1 0.1 reduce_sum.19
  42.2 0.8 copy-done.2
  43.1 0.8 fusion.1
  43.9 0.1 broadcast_in_dim.21
  43.9 16.2 %all_to_all.32 = bf16[8,16,3584]{2,1,0:T(8,128)(2,1)S(1)} all-to-all(bf16[8,16,3584]{2,1,0:T(8,128)(2,1)S(1)} %broadcast_in_dim.21), channel_id=1, replica_groups=mesh['gx'=4,'gy'=4,'gz'=8] {'gz'}, dimensions={0} | all-to-all | bytes 1835008 | tf_op jit(solution)/shard_map/all_to_all | solution.py:13
  60.2 6.9 %stack.3 = bf16[16,128,3584]{2,1,0:T(8,128)(2,1)} broadcast(bf16[128,3584]{1,0:T(8,128)(2,1)S(1)} %bitcast.20), dimensions={1,2} | broadcast | bytes 15597568 | tf_op jit(solution)/shard_map/stack | solution.py:42
  67.0 171.5 %all_to_all.33 = bf16[16,128,3584]{2,1,0:T(8,128)(2,1)S(1)} all-to-all(bf16[16,128,3584]{2,1,0:T(8,128)(2,1)} %stack.3), channel_id=1, replica_groups=mesh['gx'=4,'gy'=4,'gz'=8] {'gx','gy'}, dimensions={0} | all-to-all | bytes 29360128 | tf_op jit(solution)/shard_map/all_to_all | solution.py:42
  238.6 5.5 %copy.20 = bf16[2048,3584]{1,0:T(8,128)(2,1)} copy(bf16[2048,3584]{1,0:T(8,128)(2,1)S(1)} %bitcast.18) | data formatting | bytes 29360128
  (1 shorter events, 0.0 us)
Async XLA Ops:
  0.6 10.3 %copy-start = (f32[128,3584]{1,0:T(8,128)S(1)}, f32[128,3584]{1,0:T(8,128)}, u32[]{:S(2)}) copy-start(f32[128,3584]{1,0:T(8,128)} %param.5) | copy-start | bytes 5505028
  0.6 10.3 %copy-start.1 = (bf16[1,128,3584]{2,1,0:T(8,128)(2,1)S(1)}, bf16[1,128,3584]{2,1,0:T(8,128)(2,1)}, u32[]{:S(2)}) copy-start(bf16[1,128,3584]{2,1,0:T(8,128)(2,1)} %param.4) | copy-start | bytes 2752516
  2.5 15.1 %all-to-all-start.1 = ((bf16[8,16,448]{2,1,0:T(8,128)(2,1)}), bf16[8,16,448]{2,1,0:T(8,128)(2,1)S(1)}, u32[]{:S(2)}, u32[]{:S(2)}) async-start(bf16[8,16,448]{2,1,0:T(8,128)(2,1)} %bitcast.2), calls=%async_computation.1 | async-start | bytes 262144 | tf_op jit(solution)/shard_map/all_to_all | solution.py:28
  17.6 19.6 %all-to-all-start = ((bf16[8,2,28672]{2,1,0:T(2,128)(2,1)}), bf16[8,2,28672]{2,1,0:T(2,128)(2,1)S(1)}, u32[]{:S(2)}, u32[]{:S(2)}) async-start(bf16[8,2,28672]{2,1,0:T(2,128)(2,1)} %reshape.37), calls=%async_computation | async-start | bytes 1835008 | tf_op jit(solution)/shard_map/all_to_all | solution.py:36
  42.1 0.9 copy-start.2
